TPU v7x, 32 devices: a whole 2x2x4 slice. The times are simulated.
32 devices in a mesh: seq: 8 (over z, y), tp: 4 (over x, core).
Axes of the slice: x: 2, y: 2, z: 4, core: 2. Of those that a mesh axis runs over, the one named last changes fastest.
Arguments:
- latents: bfloat16 [1024, 3072], P('seq', 'tp'), may hold values from -6 to 6
- lengths: int32 [2], replicated, may hold values from 1 to 768, 1024 in all
- t_index: int32 [2], replicated, may hold values from 0 to 6
- mod_scale: float32 [3072], replicated, may hold values from -2 to 2
- q_weight: bfloat16 [3072, 2048], P(None, 'tp'), may hold values from -0.109375 to 0.109375
- k_weight: bfloat16 [3072, 2048], P(None, 'tp'), may hold values from -0.109375 to 0.109375
- v_weight: bfloat16 [3072, 2048], P(None, 'tp'), may hold values from -0.109375 to 0.109375
- out_weight: bfloat16 [2048, 3072], P('tp'), may hold values from -0.1875 to 0.1875
- q_gain: float32 [128], replicated, may hold values from 0.6 to 2.4
- k_gain: float32 [128], replicated, may hold values from 0.6 to 2.4
- student_weight: bfloat16 [3072, 3072], P('tp'), may hold values from -0.15625 to 0.15625
Outputs:
- target: bfloat16 [1024, 3072], P('seq', 'tp')
- student_velocity: bfloat16 [1024, 3072], P('seq', 'tp')
- loss: float32 [], replicated
Inputs may be any that keep to these rules, and one draw needn't show every extreme that they name: lengths sum to 1024.
All inputs are finite; a program needn't handle non-finite values.
Results may differ from a plain program's by a relative error of at most 0.024.
Values may be sent and summed in bfloat16 or wider, within the bound.
No kernel may reach another device: no remote copies, remote signals or barrier semaphores. Data moves between devices by JAX's collectives and lax.ppermute only.
A program may use at most 64 MiB of HBM per device.

v0:
```python
import math
import jax
import jax.numpy as jnp
from jax import lax
from jax.sharding import PartitionSpec as P

TGRID = 8
epsilon = 1e-06
kinetic_weight = 0.1


def image_index(positions, image_ends):
    return jnp.sum((positions[:, None] >= image_ends[None, :]).astype(jnp.int32), axis=1)


def head_norm(projected, gain):
    shaped = projected.reshape(projected.shape[0], -1, gain.shape[0])
    normed = shaped * lax.rsqrt(jnp.mean(shaped * shaped, axis=-1, keepdims=True) + epsilon) * gain
    return normed.astype(jnp.bfloat16)


def teacher(
    state, times, query_image, image_ends, mod_scale, q_weight, k_weight, v_weight, q_gain, k_gain
):
    row_count = state.shape[0]
    head_dim = q_gain.shape[0]
    state32 = state.astype(jnp.float32)
    normed = state32 * lax.rsqrt(jnp.mean(state32 * state32, axis=1, keepdims=True) + epsilon)
    hidden = (normed * (1.0 + times[:, None] * mod_scale[None, :])).astype(jnp.bfloat16)
    queries = head_norm(jnp.dot(hidden, q_weight, preferred_element_type=jnp.float32), q_gain)
    key_rows = head_norm(jnp.dot(hidden, k_weight, preferred_element_type=jnp.float32), k_gain)
    key_rows = key_rows.reshape(row_count, -1)
    value_rows = jnp.dot(hidden, v_weight, preferred_element_type=jnp.float32).astype(jnp.bfloat16)
    heads_here = queries.shape[1]
    score_scale = 1.0 / math.sqrt(head_dim)

    def attend(carry, key_block, value_block):
        running_max, running_total, running_sum = carry
        count = key_block.shape[0]
        key_image = image_index(jnp.arange(count, dtype=jnp.int32), image_ends)
        key_heads = key_block.reshape(count, heads_here, head_dim)
        value_heads = value_block.reshape(count, heads_here, head_dim)
        same_image = (query_image[:, None] == key_image[None, :])[:, None, :]
        scores = (
            jnp.einsum("qhd,khd->qhk", queries, key_heads, preferred_element_type=jnp.float32)
            * score_scale
        )
        scores = jnp.where(same_image, scores, -1e30)
        new_max = jnp.maximum(running_max, jnp.max(scores, axis=2))
        weights = jnp.where(same_image, jnp.exp(scores - new_max[:, :, None]), 0.0)
        new_total = jnp.sum(weights, axis=2)
        product = jnp.einsum(
            "qhk,khd->qhd",
            weights.astype(jnp.bfloat16),
            value_heads,
            preferred_element_type=jnp.float32,
        )
        return (new_max, new_total, product)

    start_carry = (
        jnp.full((row_count, heads_here), -1e30, jnp.float32),
        jnp.zeros((row_count, heads_here), jnp.float32),
        jnp.zeros((row_count, heads_here, head_dim), jnp.float32),
    )
    offset = jnp.int32(0)
    key_block = lax.all_gather(key_rows, "seq", axis=0, tiled=True)
    value_block = lax.all_gather(value_rows, "seq", axis=0, tiled=True)
    count = key_block.shape[0]
    first_image = image_index(jnp.reshape(offset, (1,)), image_ends)[0]
    last_image = image_index(jnp.reshape(offset + count - 1, (1,)), image_ends)[0]
    touches = jnp.logical_and(first_image <= query_image[-1], last_image >= query_image[0])
    final_max, final_total, final_sum = lax.cond(
        touches,
        lambda inner: attend(inner, key_block, value_block),
        lambda inner: inner,
        start_carry,
    )
    mixed = (final_sum / final_total[:, :, None]).astype(jnp.bfloat16).reshape(row_count, -1)
    return (mixed, hidden)


def on_device(
    latents,
    lengths,
    t_index,
    mod_scale,
    q_weight,
    k_weight,
    v_weight,
    out_weight,
    q_gain,
    k_gain,
    student_weight,
):
    row_count, width_here = latents.shape
    tp_index = lax.axis_index("tp")
    image_ends = jnp.cumsum(lengths)
    row_offset = lax.axis_index("seq") * row_count
    query_image = image_index(row_offset + jnp.arange(row_count, dtype=jnp.int32), image_ends)
    one_hot = (
        query_image[:, None] == jnp.arange(lengths.shape[0], dtype=jnp.int32)[None, :]
    ).astype(jnp.float32)
    start_times = jnp.sum(one_hot * (t_index.astype(jnp.float32) / TGRID)[None, :], axis=1)
    step_size = 1.0 / TGRID
    whole_rows = lax.all_gather(latents, "tp", axis=1, tiled=True)
    velocities = []
    first_hidden = whole_rows
    state_shard = latents
    for euler_index in range(2):
        if euler_index == 1:
            whole_rows = lax.all_gather(state_shard, "tp", axis=1, tiled=True)
        mixed, hidden = teacher(
            whole_rows,
            start_times + euler_index * step_size,
            query_image,
            image_ends,
            mod_scale,
            q_weight,
            k_weight,
            v_weight,
            q_gain,
            k_gain,
        )
        if euler_index == 0:
            first_hidden = hidden
        partial_value = jnp.dot(mixed, out_weight, preferred_element_type=jnp.float32)
        velocity = lax.psum_scatter(
            partial_value.astype(jnp.bfloat16), "tp", scatter_dimension=1, tiled=True
        )
        velocities.append(velocity)
        state_shard = (
            latents.astype(jnp.float32) + step_size * velocity.astype(jnp.float32)
        ).astype(jnp.bfloat16)
    columns = lax.dynamic_slice_in_dim(first_hidden, tp_index * width_here, width_here, 1)
    student_terms = jnp.dot(columns, student_weight, preferred_element_type=jnp.float32)
    student_velocity = lax.psum_scatter(
        student_terms.astype(jnp.bfloat16), "tp", scatter_dimension=1, tiled=True
    )
    target = (0.5 * (velocities[0].astype(jnp.float32) + velocities[1].astype(jnp.float32))).astype(
        jnp.bfloat16
    )
    student32 = student_velocity.astype(jnp.float32)
    residual = student32 - target.astype(jnp.float32)
    per_token = jnp.sum(residual * residual, axis=1) + kinetic_weight * jnp.sum(
        student32 * student32, axis=1
    )
    image_part = jnp.sum(one_hot * per_token[:, None], axis=0)
    image_sum = lax.psum(image_part, ("seq", "tp"))
    loss = jnp.mean(image_sum / (lengths.astype(jnp.float32) * mod_scale.shape[0]))
    return (target, student_velocity, loss)


def solution(mesh):
    placed = (
        P("seq", "tp"),
        P(),
        P(),
        P(),
        P(None, "tp"),
        P(None, "tp"),
        P(None, "tp"),
        P("tp", None),
        P(),
        P(),
        P("tp", None),
    )
    return jax.shard_map(
        on_device,
        mesh=mesh,
        in_specs=placed,
        out_specs=(P("seq", "tp"), P("seq", "tp"), P()),
        check_vma=False,
    )
```

profile of v0, /device:TPU:0, one launch (start us, length us, event | category | flops | bytes accessed | tf_op | source)
XLA Modules:
  0.0 336.3 jit_solution(12734759485271382639)
XLA Ops:
  8.1 10.4 %all_gather.18 = bf16[128,3072]{1,0:T(8,128)(2,1)S(1)} all-gather(bf16[128,768]{1,0:T(8,128)(2,1)} %param.15), channel_id=1, replica_groups=mesh['seq'=8,'tp'=4] {'tp'}, dimensions={1}, use_global_device_ids=true | all-gather | bytes 983040 | tf_op jit(solution)/shard_map/all_gather | solution.py:105
  23.6 3.1 convolution_convert_fusion.4
  26.8 3.4 %fusion.70 = (f32[128,512]{1,0:T(8,128)}, f32[128,512]{1,0:T(8,128)S(1)}) fusion(bf16[128,3072]{1,0:T(8,128)(2,1)} %copy-done.1, bf16[3072,512]{1,0:T(8,128)(2,1)} %param.20), kind=kOutput, calls=%fused_computation.115 | convolution fusion | flops 402718720 | bytes 4456448 | tf_op jit(solution)/shard_map/dot_general | solution.py:31
  30.2 1.8 mul.218
  38.0 2.7 fusion.72
  42.9 25.1 %all-gather.7.cloned.1.call-done = bf16[1024,512]{1,0:T(8,128)(2,1)} async-done(((bf16[128,512]{1,0:T(8,128)(2,1)}), bf16[1024,512]{1,0:T(8,128)(2,1)}) %all-gather.7.cloned.1.call-update) | async-done | bytes 1048592 | tf_op jit(solution)/shard_map/all_gather | solution.py:67
  68.0 41.7 %all-gather.5.cloned.1.call-done = bf16[1024,512]{1,0:T(8,128)(2,1)} async-done(((bf16[128,512]{1,0:T(8,128)(2,1)}), bf16[1024,512]{1,0:T(8,128)(2,1)}) %all-gather.5.cloned.1.call-update) | async-done | bytes 1048592 | tf_op jit(solution)/shard_map/all_gather | solution.py:66
  109.7 6.0 %conditional.2 = (f32[128,4]{0,1:T(4,128)S(1)}, f32[128,4,128]{0,2,1:T(8,128)S(1)}) conditional(s32[]{:T(128)} %convert_element_type.124, () %tuple.24, (s32[128]{0:T(128)S(1)}, s32[2]{0:T(128)}, bf16[1024,512]{1,0:T(8,128)(2,1)}, bf16[128,4,128]{2,0,1:T(8,128)(2,1)S(1)}, bf16[1024,512]{1,0:T(8,128)(2,1)}) %tuple.59), branch_computations={%region_8.9_spmd, %region_9.13_spmd} | conditional | flops 275386880 | bytes 14045748 | solution.py:72
  110.7 1.7 fusion
  117.4 22.0 %reduce-scatter.4.cloned.1.call-done = bf16[128,768]{1,0:T(8,128)(2,1)} async-done(((bf16[128,3072]{1,0:T(8,128)(2,1)}), bf16[128,768]{1,0:T(8,128)(2,1)}) %reduce-scatter.4.cloned.1.call-update) | async-done | bytes 196624 | tf_op jit(solution)/shard_map/reduce_scatter | solution.py:127
  140.4 8.0 %all_gather.21 = bf16[128,3072]{1,0:T(8,128)(2,1)S(1)} all-gather(bf16[128,768]{1,0:T(8,128)(2,1)S(1)} %fusion.43), channel_id=1, replica_groups=mesh['seq'=8,'tp'=4] {'tp'}, dimensions={1}, use_global_device_ids=true | all-gather | bytes 983040 | tf_op jit(solution)/shard_map/all_gather | solution.py:111
  149.3 3.2 convolution_convert_fusion.3
  152.6 3.6 %fusion.71 = (f32[128,512]{1,0:T(8,128)}, f32[128,512]{1,0:T(8,128)}) fusion(bf16[3072,512]{1,0:T(8,128)(2,1)} %param.20, bf16[128,3072]{1,0:T(8,128)(2,1)} %copy-done.3, f32[128]{0:T(128)S(1)} %broadcast_add_fusion, f32[128]{0:T(128)S(1)} %add_rsqrt_fusion.4, f32[3072]{0:T(1024)S(1)} %copy-done.6), kind=kOutput, calls=%fused_computation.116 | convolution fusion | flops 405078016 | bytes 4469760 | tf_op jit(solution)/shard_map/dot_general | solution.py:31
  157.6 1.6 fusion.50
  159.4 4.2 %convolution_convert_fusion.2 = bf16[128,3072]{1,0:T(8,128)(2,1)} fusion(bf16[768,3072]{1,0:T(8,128)(2,1)} %param.25, bf16[128,3072]{1,0:T(8,128)(2,1)} %copy-done.1, s32[]{:T(128)S(6)} %select_n.16), kind=kOutput, calls=%fused_computation.48 | convolution fusion | flops 604372992 | bytes 5701636 | tf_op jit(solution)/shard_map/dot_general | solution.py:135
  163.7 3.5 %fusion.64 = f32[128,512]{1,0:T(8,128)} fusion(bf16[3072,512]{1,0:T(8,128)(2,1)} %param.19, bf16[128,3072]{1,0:T(8,128)(2,1)} %copy-done.3, f32[128]{0:T(128)S(1)} %broadcast_add_fusion, f32[128]{0:T(128)S(1)} %add_rsqrt_fusion.4, f32[3072]{0:T(1024)S(1)} %copy-done.6), kind=kOutput, calls=%fused_computation.112 | convolution fusion | flops 405012480 | bytes 4207616 | tf_op jit(solution)/shard_map/dot_general | solution.py:30
  169.6 23.9 %all-gather.11.cloned.1.call-done = bf16[1024,512]{1,0:T(8,128)(2,1)} async-done(((bf16[128,512]{1,0:T(8,128)(2,1)}), bf16[1024,512]{1,0:T(8,128)(2,1)}) %all-gather.11.cloned.1.call-update) | async-done | bytes 1048592 | tf_op jit(solution)/shard_map/all_gather | solution.py:67
  193.5 41.6 %all-gather.9.cloned.1.call-done = bf16[1024,512]{1,0:T(8,128)(2,1)} async-done(((bf16[128,512]{1,0:T(8,128)(2,1)}), bf16[1024,512]{1,0:T(8,128)(2,1)}) %all-gather.9.cloned.1.call-update) | async-done | bytes 1048592 | tf_op jit(solution)/shard_map/all_gather | solution.py:66
  235.1 5.3 %conditional.3 = (f32[128,4]{0,1:T(4,128)S(1)}, f32[128,4,128]{0,2,1:T(8,128)S(1)}) conditional(s32[]{:T(128)} %convert_element_type.124, () %tuple.26, (s32[128]{0:T(128)S(1)}, s32[2]{0:T(128)S(1)}, bf16[1024,512]{1,0:T(8,128)(2,1)}, bf16[128,4,128]{2,0,1:T(8,128)(2,1)S(1)}, bf16[1024,512]{1,0:T(8,128)(2,1)}) %tuple.60), branch_computations={%region_17.18_spmd, %region_18.0_spmd} | conditional | flops 275386880 | bytes 14045748 | solution.py:72
  235.4 1.8 fusion.18
  242.0 18.1 %reduce-scatter.8.cloned.1.call-done = bf16[128,768]{1,0:T(8,128)(2,1)} async-done(((bf16[128,3072]{1,0:T(8,128)(2,1)}), bf16[128,768]{1,0:T(8,128)(2,1)}) %reduce-scatter.8.cloned.1.call-update) | async-done | bytes 196624 | tf_op jit(solution)/shard_map/reduce_scatter | solution.py:136
  260.0 25.8 %reduce-scatter.6.cloned.1.call-done = bf16[128,768]{1,0:T(8,128)(2,1)} async-done(((bf16[128,3072]{1,0:T(8,128)(2,1)}), bf16[128,768]{1,0:T(8,128)(2,1)}) %reduce-scatter.6.cloned.1.call-update) | async-done | bytes 196624 | tf_op jit(solution)/shard_map/reduce_scatter | solution.py:127
  285.8 1.8 fusion.48
  287.8 39.3 %psum.7 = f32[2]{0:T(128)S(1)} all-reduce(f32[2]{0:T(128)S(1)} %select_reduce_fusion), channel_id=1, replica_groups=mesh['seq'=8,'tp'=4] {'seq','tp'}, use_global_device_ids=true, to_apply=%region_27.28 | all-reduce | flops 2 | bytes 16 | tf_op jit(solution)/shard_map/psum | solution.py:148
  (98 shorter events, 29.2 us)
Async XLA Ops:
  7.2 108.6 %copy-start = (bf16[512,3072]{1,0:T(8,128)(2,1)S(1)}, bf16[512,3072]{1,0:T(8,128)(2,1)}, u32[]{:S(2)}) copy-start(bf16[512,3072]{1,0:T(8,128)(2,1)} %param.22) | copy-start | bytes 9437188
  7.2 60.8 %all-gather.7.cloned.1.call-start = ((), (), s32[]{:S(2)}) async-start(), calls=%async_computation.4 | async-start | bytes 1179648 | tf_op jit(solution)/shard_map/all_gather | solution.py:67
  18.5 0.9 copy-start.2
  20.4 14.4 %copy-start.8 = (s32[2,1]{0,1:T(1,128)}, s32[2,1]{0,1:T(1,128)S(1)}, u32[]{:S(2)}) copy-start(s32[2,1]{0,1:T(1,128)S(1)} %reduce-window.4) | copy-start | bytes 28
  20.6 0.6 copy-start.10
  22.7 0.9 copy-start.1
  26.7 6.4 %copy-start.12 = (f32[128]{0:T(128)S(1)}, f32[128]{0:T(128)}, u32[]{:S(2)}) copy-start(f32[128]{0:T(128)} %param.24) | copy-start | bytes 1540
  26.7 83.0 %all-gather.5.cloned.1.call-start = ((), (), s32[]{:S(2)}) async-start(), calls=%async_computation.3 | async-start | bytes 1179648 | tf_op jit(solution)/shard_map/all_gather | solution.py:66
  34.1 105.3 %reduce-scatter.4.cloned.1.call-start = ((), (), s32[]{:S(2)}) async-start(), calls=%async_computation.5 | async-start | bytes 983040 | tf_op jit(solution)/shard_map/reduce_scatter | solution.py:127
  38.0 4.8 %copy-start.7 = (f32[128]{0:T(128)S(1)}, f32[128]{0:T(128)}, u32[]{:S(2)}) copy-start(f32[128]{0:T(128)} %param.23) | copy-start | bytes 1540
  109.7 2.8 copy-start.14
  115.8 1.6 copy-start.11
  115.8 23.6 %copy-start.5 = (bf16[128,768]{1,0:T(8,128)(2,1)S(1)}, bf16[128,768]{1,0:T(8,128)(2,1)}, u32[]{:S(2)}) copy-start(bf16[128,768]{1,0:T(8,128)(2,1)} %param.15) | copy-start | bytes 589828
  117.3 32.0 %copy-start.6 = (f32[3072]{0:T(1024)S(1)}, f32[3072]{0:T(1024)}, u32[]{:S(2)}) copy-start(f32[3072]{0:T(1024)} %param.18) | copy-start | bytes 36868
  117.3 76.2 %all-gather.11.cloned.1.call-start = ((), (), s32[]{:S(2)}) async-start(), calls=%async_computation.7 | async-start | bytes 1179648 | tf_op jit(solution)/shard_map/all_gather | solution.py:67
  148.4 0.9 copy-start.3
  152.5 82.5 %all-gather.9.cloned.1.call-start = ((), (), s32[]{:S(2)}) async-start(), calls=%async_computation.6 | async-start | bytes 1179648 | tf_op jit(solution)/shard_map/all_gather | solution.py:66
  159.3 100.7 %reduce-scatter.8.cloned.1.call-start = ((), (), s32[]{:S(2)}) async-start(), calls=%async_computation.9 | async-start | bytes 983040 | tf_op jit(solution)/shard_map/reduce_scatter | solution.py:136
  163.6 122.2 %reduce-scatter.6.cloned.1.call-start = ((), (), s32[]{:S(2)}) async-start(), calls=%async_computation.8 | async-start | bytes 983040 | tf_op jit(solution)/shard_map/reduce_scatter | solution.py:127
  163.7 71.4 %copy-start.9 = (s32[2,1]{0,1:T(1,128)S(1)}, s32[2,1]{0,1:T(1,128)}, u32[]{:S(2)}) copy-start(s32[2,1]{0,1:T(1,128)} %copy-done.8) | copy-start | bytes 28
  235.1 2.1 copy-start.13
  240.4 45.4 %copy-start.4 = (bf16[128,768]{1,0:T(8,128)(2,1)S(1)}, bf16[128,768]{1,0:T(8,128)(2,1)}, u32[]{:S(2)}) copy-start(bf16[128,768]{1,0:T(8,128)(2,1)} %reduce-scatter.4.cloned.1.call-done) | copy-start | bytes 589828
  240.4 86.6 %copy-start.15 = (s32[2]{0:T(128)S(1)}, s32[2]{0:T(128)}, u32[]{:S(2)}) copy-start(s32[2]{0:T(128)} %param.16) | copy-start | bytes 28
Sparse Core Ops, SparseCore 0:
  26.8 41.1 all-gather.6
  70.7 38.9 all-gather.4
  117.4 21.9 reduce-scatter.3
  152.6 40.8 all-gather.10
  196.0 38.9 all-gather.8
  238.0 21.9 reduce-scatter.7
  262.5 23.2 reduce-scatter.5
where the time goes:
time: 337 us; the launch traced here: 336 us
  waiting for transfers between devices  198 us (59%)
  blocking collectives  57.7 us (17%)
  matrix products  33.4 us (10%)
  between operations  18.7 us (6%)
  other arithmetic  16.8 us (5%)
  local copies, waits for them, and re-layouts  11 us (3%)
    all_gather x2, waiting for transfers between devices, teacher(): key_block = lax.all_gather(key_rows, 'seq', axis=0, tiled=True)  83.3 us
    all_gather x2, waiting for transfers between devices, teacher(): value_block = lax.all_gather(value_rows, 'seq', axis=0, tiled=True)  49 us
    reduce_scatter x2, waiting for transfers between devices, on_device(): lax.psum_scatter(partial_value.astype(jnp.bfloat16), 'tp', scatter_dimens...  47.8 us
    psum x1, blocking collectives, on_device(): image_sum = lax.psum(image_part, ('seq', 'tp'))  39.3 us
    reduce_scatter x1, waiting for transfers between devices, on_device(): lax.psum_scatter(student_terms.astype(jnp.bfloat16), 'tp', scatter_dimens...  18.1 us
    all_gather x1, blocking collectives, on_device(): whole_rows = lax.all_gather(latents, 'tp', axis=1, tiled=True)  10.4 us
    all_gather x1, blocking collectives, on_device(): whole_rows = lax.all_gather(state_shard, 'tp', axis=1, tiled=True)  8.03 us
    dot_general x2, matrix products, teacher(): jnp.dot(hidden, k_weight, preferred_element_type=jnp.float32)  7.02 us
  transfers between devices with their start and end apart: 7, of which 7 were waited for; matrix products, arithmetic and copies ran while one was open for 11% of the time, Pallas kernels for 0%

commit v1 on v0

--- a/solution.py
+++ b/solution.py
@@ -7,6 +7,16 @@
 TGRID = 8
 epsilon = 1e-06
 kinetic_weight = 0.1
+
+
+def around_the_ring(x, mesh_axis, dim):
+    count = lax.axis_size(mesh_axis)
+    held, shards = (x, [x])
+    for _ in range(count - 1):
+        held = lax.ppermute(held, mesh_axis, [(i, (i + 1) % count) for i in range(count)])
+        shards.insert(0, held)
+    line = jnp.concatenate(shards, axis=dim)
+    return jnp.roll(line, (lax.axis_index(mesh_axis) + 1) * x.shape[dim], axis=dim)
 
 
 def image_index(positions, image_ends):
@@ -63,7 +73,7 @@
         jnp.zeros((row_count, heads_here, head_dim), jnp.float32),
     )
     offset = jnp.int32(0)
-    key_block = lax.all_gather(key_rows, "seq", axis=0, tiled=True)
+    key_block = around_the_ring(key_rows, "seq", 0)
     value_block = lax.all_gather(value_rows, "seq", axis=0, tiled=True)
     count = key_block.shape[0]
     first_image = image_index(jnp.reshape(offset, (1,)), image_ends)[0]

time: 337 us -> 284 us (0.84)
  waiting for transfers between devices: 198 us -> 127 us
  local copies, waits for them, and re-layouts: 11 us -> 21.5 us
  other arithmetic: 16.8 us -> 20.4 us
    ppermute x0 -> x14, waiting for transfers between devices: none -> 84.9 us  [around_the_ring(): lax.ppermute(held, mesh_axis, [(i, (i + 1) % count) for i in range(count)])]
    all_gather x2 -> x0, waiting for transfers between devices: 83.3 us -> none  [teacher(): key_block = lax.all_gather(key_rows, 'seq', axis=0, tiled=True)]
    all_gather x2, waiting for transfers between devices: 49 us -> 0.01 us  [teacher(): value_block = lax.all_gather(value_rows, 'seq', axis=0, tiled=True)]
    reduce_scatter x1, waiting for transfers between devices: 18.1 us -> 0.02 us  [on_device(): lax.psum_scatter(student_terms.astype(jnp.bfloat16), 'tp', scatter_dimens...]
    unnamed x28 -> x64, local copies, waits for them, and re-layouts: 3.05 us -> 11.2 us
    reduce_scatter x2, waiting for transfers between devices: 47.8 us -> 42.2 us  [on_device(): lax.psum_scatter(partial_value.astype(jnp.bfloat16), 'tp', scatter_dimens...]
  transfers between devices with their start and end apart: 7 -> 19, of which waited for: 7 -> 16; matrix products, arithmetic and copies ran while one was open for 11% -> 17% of each run, Pallas kernels for 0% -> 0%
where the time goes in v1:
time: 284 us; the launch traced here: 283 us
  waiting for transfers between devices  127 us (45%)
  blocking collectives  57.6 us (20%)
  matrix products  33.9 us (12%)
  local copies, waits for them, and re-layouts  21.5 us (8%)
  other arithmetic  20.4 us (7%)
  between operations  18.5 us (7%)
  starting transfers between devices  3.34 us (1%)
    ppermute x14, waiting for transfers between devices, around_the_ring(): lax.ppermute(held, mesh_axis, [(i, (i + 1) % count) for i in range(count)])  84.9 us
    reduce_scatter x2, waiting for transfers between devices, on_device(): lax.psum_scatter(partial_value.astype(jnp.bfloat16), 'tp', scatter_dimens...  42.2 us
    psum x1, blocking collectives, on_device(): image_sum = lax.psum(image_part, ('seq', 'tp'))  39.3 us
    unnamed x64, local copies, waits for them, and re-layouts  11.2 us
    all_gather x1, blocking collectives, on_device(): whole_rows = lax.all_gather(latents, 'tp', axis=1, tiled=True)  10.3 us
    all_gather x1, blocking collectives, on_device(): whole_rows = lax.all_gather(state_shard, 'tp', axis=1, tiled=True)  8.01 us
    dot_general x2, matrix products, teacher(): jnp.dot(hidden, k_weight, preferred_element_type=jnp.float32)  7.03 us
    dot_general x2, matrix products, teacher(): jnp.dot(hidden, v_weight, preferred_element_type=jnp.float32)  6.56 us
  transfers between devices with their start and end apart: 19, of which 16 were waited for; matrix products, arithmetic and copies ran while one was open for 17% of the time, Pallas kernels for 0%

profile of v1, /device:TPU:0, one launch (start us, length us, event | category | flops | bytes accessed | tf_op | source)
XLA Modules:
  0.0 282.6 jit_solution(15101647290203145334)
XLA Ops:
  8.8 10.3 %all_gather.12 = bf16[128,3072]{1,0:T(8,128)(2,1)S(1)} all-gather(bf16[128,768]{1,0:T(8,128)(2,1)} %param.17), channel_id=1, replica_groups=mesh['seq'=8,'tp'=4] {'tp'}, dimensions={1}, use_global_device_ids=true | all-gather | bytes 983040 | tf_op jit(solution)/shard_map/all_gather | solution.py:115
  22.7 3.5 %fusion.70 = (f32[128,512]{1,0:T(8,128)}, f32[128,512]{1,0:T(8,128)S(1)}) fusion(bf16[128,3072]{1,0:T(8,128)(2,1)S(1)} %fusion.38, bf16[3072,512]{1,0:T(8,128)(2,1)} %param.22), kind=kOutput, calls=%fused_computation.135 | convolution fusion | flops 402718720 | bytes 4456448 | tf_op jit(solution)/shard_map/dot_general | solution.py:41
  30.9 7.0 %collective-permute-done = bf16[128,512]{1,0:T(8,128)(2,1)S(1)} collective-permute-done((bf16[128,512]{1,0:T(8,128)(2,1)S(1)}, bf16[128,512]{1,0:T(8,128)(2,1)S(1)}, u32[]{:S(2)}, u32[]{:S(2)}) %collective-permute-start) | collective-permute-done | bytes 131104 | tf_op jit(solution)/shard_map/ppermute | solution.py:16
  38.6 7.7 %collective-permute-done.1 = bf16[128,512]{1,0:T(8,128)(2,1)S(1)} collective-permute-done((bf16[128,512]{1,0:T(8,128)(2,1)S(1)}, bf16[128,512]{1,0:T(8,128)(2,1)S(1)}, u32[]{:S(2)}, u32[]{:S(2)}) %collective-permute-start.1) | collective-permute-done | bytes 131104 | tf_op jit(solution)/shard_map/ppermute | solution.py:16
  46.3 3.4 %convolution_convert_fusion.4 = bf16[128,512]{1,0:T(8,128)(2,1)} fusion(bf16[128,3072]{1,0:T(8,128)(2,1)} %copy-done.1, bf16[3072,512]{1,0:T(8,128)(2,1)} %param.23), kind=kOutput, calls=%fused_computation.64 | convolution fusion | flops 402718720 | bytes 4063232 | tf_op jit(solution)/shard_map/dot_general | solution.py:43
  49.8 4.3 %collective-permute-done.2 = bf16[128,512]{1,0:T(8,128)(2,1)} collective-permute-done((bf16[128,512]{1,0:T(8,128)(2,1)S(1)}, bf16[128,512]{1,0:T(8,128)(2,1)}, u32[]{:S(2)}, u32[]{:S(2)}) %collective-permute-start.2) | collective-permute-done | bytes 131104 | tf_op jit(solution)/shard_map/ppermute | solution.py:16
  57.4 4.7 %collective-permute-done.3 = bf16[128,512]{1,0:T(8,128)(2,1)} collective-permute-done((bf16[128,512]{1,0:T(8,128)(2,1)}, bf16[128,512]{1,0:T(8,128)(2,1)}, u32[]{:S(2)}, u32[]{:S(2)}) %collective-permute-start.3) | collective-permute-done | bytes 131104 | tf_op jit(solution)/shard_map/ppermute | solution.py:16
  70.4 7.9 %collective-permute-done.5 = bf16[128,512]{1,0:T(8,128)(2,1)S(1)} collective-permute-done((bf16[128,512]{1,0:T(8,128)(2,1)}, bf16[128,512]{1,0:T(8,128)(2,1)S(1)}, u32[]{:S(2)}, u32[]{:S(2)}) %collective-permute-start.5) | collective-permute-done | bytes 131104 | tf_op jit(solution)/shard_map/ppermute | solution.py:16
  79.1 8.8 %collective-permute-done.6 = bf16[128,512]{1,0:T(8,128)(2,1)S(1)} collective-permute-done((bf16[128,512]{1,0:T(8,128)(2,1)S(1)}, bf16[128,512]{1,0:T(8,128)(2,1)S(1)}, u32[]{:S(2)}, u32[]{:S(2)}) %collective-permute-start.6) | collective-permute-done | bytes 131104 | tf_op jit(solution)/shard_map/ppermute | solution.py:16
  94.0 5.4 %conditional.2 = (f32[128,4]{0,1:T(4,128)S(1)}, f32[128,4,128]{0,2,1:T(8,128)S(1)}) conditional(s32[]{:T(128)} %convert_element_type.124, () %tuple.25, (s32[128]{0:T(128)S(1)}, s32[2]{0:T(128)S(1)}, bf16[2048,512]{1,0:T(8,128)(2,1)}, bf16[128,4,128]{2,0,1:T(8,128)(2,1)}, bf16[1024,512]{1,0:T(8,128)(2,1)}, /*index=5*/s32[]{:T(128)}) %tuple.61), branch_computations={%region_8.10_spmd, %region_9.14_spmd.clone} | conditional | flops 275386880 | bytes 14046260 | solution.py:82
  101.1 21.7 %reduce-scatter.4.cloned.1.call-done = bf16[128,768]{1,0:T(8,128)(2,1)} async-done(((bf16[128,3072]{1,0:T(8,128)(2,1)}), bf16[128,768]{1,0:T(8,128)(2,1)}) %reduce-scatter.4.cloned.1.call-update) | async-done | bytes 196624 | tf_op jit(solution)/shard_map/reduce_scatter | solution.py:137
  123.9 8.0 %all_gather.14 = bf16[128,3072]{1,0:T(8,128)(2,1)S(1)} all-gather(bf16[128,768]{1,0:T(8,128)(2,1)S(1)} %fusion.43), channel_id=1, replica_groups=mesh['seq'=8,'tp'=4] {'tp'}, dimensions={1}, use_global_device_ids=true | all-gather | bytes 983040 | tf_op jit(solution)/shard_map/all_gather | solution.py:121
  136.0 3.6 %fusion.71 = (f32[128,512]{1,0:T(8,128)}, f32[128,512]{1,0:T(8,128)}) fusion(bf16[3072,512]{1,0:T(8,128)(2,1)} %param.22, bf16[128,3072]{1,0:T(8,128)(2,1)} %copy-done.3, f32[128]{0:T(128)S(1)} %broadcast_add_fusion, f32[128]{0:T(128)S(1)} %add_rsqrt_fusion.4, f32[3072]{0:T(1024)S(1)} %copy-done.12), kind=kOutput, calls=%fused_computation.136 | convolution fusion | flops 405078016 | bytes 4469760 | tf_op jit(solution)/shard_map/dot_general | solution.py:41
  143.6 7.8 %collective-permute-done.7 = bf16[128,512]{1,0:T(8,128)(2,1)S(1)} collective-permute-done((bf16[128,512]{1,0:T(8,128)(2,1)S(1)}, bf16[128,512]{1,0:T(8,128)(2,1)S(1)}, u32[]{:S(2)}, u32[]{:S(2)}) %collective-permute-start.7) | collective-permute-done | bytes 131104 | tf_op jit(solution)/shard_map/ppermute | solution.py:16
  152.1 7.9 %collective-permute-done.8 = bf16[128,512]{1,0:T(8,128)(2,1)S(1)} collective-permute-done((bf16[128,512]{1,0:T(8,128)(2,1)S(1)}, bf16[128,512]{1,0:T(8,128)(2,1)S(1)}, u32[]{:S(2)}, u32[]{:S(2)}) %collective-permute-start.8) | collective-permute-done | bytes 131104 | tf_op jit(solution)/shard_map/ppermute | solution.py:16
  159.9 7.8 %collective-permute-done.9 = bf16[128,512]{1,0:T(8,128)(2,1)S(1)} collective-permute-done((bf16[128,512]{1,0:T(8,128)(2,1)S(1)}, bf16[128,512]{1,0:T(8,128)(2,1)S(1)}, u32[]{:S(2)}, u32[]{:S(2)}) %collective-permute-start.9) | collective-permute-done | bytes 131104 | tf_op jit(solution)/shard_map/ppermute | solution.py:16
  167.8 4.2 %convolution_convert_fusion.2 = bf16[128,3072]{1,0:T(8,128)(2,1)} fusion(bf16[768,3072]{1,0:T(8,128)(2,1)} %param.27, bf16[128,3072]{1,0:T(8,128)(2,1)} %copy-done.1, s32[]{:T(128)S(6)} %select_n.26), kind=kOutput, calls=%fused_computation.50 | convolution fusion | flops 604372992 | bytes 5701636 | tf_op jit(solution)/shard_map/dot_general | solution.py:145
  172.0 4.1 %collective-permute-done.10 = bf16[128,512]{1,0:T(8,128)(2,1)} collective-permute-done((bf16[128,512]{1,0:T(8,128)(2,1)S(1)}, bf16[128,512]{1,0:T(8,128)(2,1)}, u32[]{:S(2)}, u32[]{:S(2)}) %collective-permute-start.10) | collective-permute-done | bytes 131104 | tf_op jit(solution)/shard_map/ppermute | solution.py:16
  176.1 3.5 %fusion.64 = f32[128,512]{1,0:T(8,128)} fusion(bf16[3072,512]{1,0:T(8,128)(2,1)} %param.21, bf16[128,3072]{1,0:T(8,128)(2,1)} %copy-done.3, f32[128]{0:T(128)S(1)} %copy-done.25, f32[128]{0:T(128)} %copy-done.26, f32[3072]{0:T(1024)S(1)} %copy-done.12), kind=kOutput, calls=%fused_computation.132 | convolution fusion | flops 405012480 | bytes 4207616 | tf_op jit(solution)/shard_map/dot_general | solution.py:40
  184.1 7.9 %collective-permute-done.12 = bf16[128,512]{1,0:T(8,128)(2,1)S(1)} collective-permute-done((bf16[128,512]{1,0:T(8,128)(2,1)}, bf16[128,512]{1,0:T(8,128)(2,1)S(1)}, u32[]{:S(2)}, u32[]{:S(2)}) %collective-permute-start.12) | collective-permute-done | bytes 131104 | tf_op jit(solution)/shard_map/ppermute | solution.py:16
  193.7 5.9 %collective-permute-done.13 = bf16[128,512]{1,0:T(8,128)(2,1)S(1)} collective-permute-done((bf16[128,512]{1,0:T(8,128)(2,1)S(1)}, bf16[128,512]{1,0:T(8,128)(2,1)S(1)}, u32[]{:S(2)}, u32[]{:S(2)}) %collective-permute-start.13) | collective-permute-done | bytes 131104 | tf_op jit(solution)/shard_map/ppermute | solution.py:16
  204.9 5.4 %conditional.3 = (f32[128,4]{0,1:T(4,128)S(1)}, f32[128,4,128]{0,2,1:T(8,128)S(1)}) conditional(s32[]{:T(128)} %convert_element_type.124, () %tuple.27, (s32[128]{0:T(128)S(1)}, s32[2]{0:T(128)S(1)}, bf16[2048,512]{1,0:T(8,128)(2,1)}, bf16[128,4,128]{2,0,1:T(8,128)(2,1)}, bf16[1024,512]{1,0:T(8,128)(2,1)}, /*index=5*/s32[]{:T(128)}) %tuple.62), branch_computations={%region_17.19_spmd, %region_18.23_spmd.clone} | conditional | flops 275386880 | bytes 14046260 | solution.py:82
  212.0 20.5 %reduce-scatter.6.cloned.1.call-done = bf16[128,768]{1,0:T(8,128)(2,1)} async-done(((bf16[128,3072]{1,0:T(8,128)(2,1)}), bf16[128,768]{1,0:T(8,128)(2,1)}) %reduce-scatter.6.cloned.1.call-update) | async-done | bytes 196624 | tf_op jit(solution)/shard_map/reduce_scatter | solution.py:137
  234.4 39.3 %psum.7 = f32[2]{0:T(128)S(1)} all-reduce(f32[2]{0:T(128)S(1)} %select_reduce_fusion), channel_id=1, replica_groups=mesh['seq'=8,'tp'=4] {'seq','tp'}, use_global_device_ids=true, to_apply=%region_27.29 | all-reduce | flops 2 | bytes 16 | tf_op jit(solution)/shard_map/psum | solution.py:158
  (160 shorter events, 64.4 us)
Async XLA Ops:
  7.2 92.4 %copy-start = (bf16[512,3072]{1,0:T(8,128)(2,1)S(1)}, bf16[512,3072]{1,0:T(8,128)(2,1)}, u32[]{:S(2)}) copy-start(bf16[512,3072]{1,0:T(8,128)(2,1)} %param.24) | copy-start | bytes 9437188
  7.2 86.9 %all-gather.3.cloned.1.call-start = ((), (), s32[]{:S(2)}) async-start(), calls=%async_computation.3 | async-start | bytes 1179648 | tf_op jit(solution)/shard_map/all_gather | solution.py:77
  21.0 41.1 %copy-start.16 = (s32[2,1]{0,1:T(1,128)}, s32[2,1]{0,1:T(1,128)S(1)}, u32[]{:S(2)}) copy-start(s32[2,1]{0,1:T(1,128)S(1)} %reduce-window.4) | copy-start | bytes 28
  21.1 72.9 %copy-start.13 = (s32[128]{0:T(128)}, s32[128]{0:T(128)S(1)}, u32[]{:S(2)}) copy-start(s32[128]{0:T(128)S(1)} %fusion.58) | copy-start | bytes 1540
  29.3 8.6 %collective-permute-start = (bf16[128,512]{1,0:T(8,128)(2,1)S(1)}, bf16[128,512]{1,0:T(8,128)(2,1)S(1)}, u32[]{:S(2)}, u32[]{:S(2)}) collective-permute-start(bf16[128,512]{1,0:T(8,128)(2,1)S(1)} %fusion.52), channel_id=1, source_target_pairs={{0,4},{4,8},{8,12},{12,16},{16,20},{20,24},{24,28},{28,0},{1,5},{5... | collective-permute-start | bytes 393224 | tf_op jit(solution)/shard_map/ppermute | solution.py:16
  38.6 7.7 %collective-permute-start.1 = (bf16[128,512]{1,0:T(8,128)(2,1)S(1)}, bf16[128,512]{1,0:T(8,128)(2,1)S(1)}, u32[]{:S(2)}, u32[]{:S(2)}) collective-permute-start(bf16[128,512]{1,0:T(8,128)(2,1)S(1)} %collective-permute-done), channel_id=1, source_target_pairs={{0,4},{4,8},{8,12},{12,16},{16,20},{20,24},{24,28},{28,0},{1,5},{5... | collective-permute-start | bytes 393224 | tf_op jit(solution)/shard_map/ppermute | solution.py:16
  46.3 7.8 %collective-permute-start.2 = (bf16[128,512]{1,0:T(8,128)(2,1)S(1)}, bf16[128,512]{1,0:T(8,128)(2,1)}, u32[]{:S(2)}, u32[]{:S(2)}) collective-permute-start(bf16[128,512]{1,0:T(8,128)(2,1)S(1)} %collective-permute-done.1), channel_id=1, source_target_pairs={{0,4},{4,8},{8,12},{12,16},{16,20},{20,24},{24,28},{28,0},{1,5},{5... | collective-permute-start | bytes 393224 | tf_op jit(solution)/shard_map/ppermute | solution.py:16
  49.8 73.1 %reduce-scatter.4.cloned.1.call-start = ((), (), s32[]{:S(2)}) async-start(), calls=%async_computation.4 | async-start | bytes 983040 | tf_op jit(solution)/shard_map/reduce_scatter | solution.py:137
  54.1 8.0 %collective-permute-start.3 = (bf16[128,512]{1,0:T(8,128)(2,1)}, bf16[128,512]{1,0:T(8,128)(2,1)}, u32[]{:S(2)}, u32[]{:S(2)}) collective-permute-start(bf16[128,512]{1,0:T(8,128)(2,1)} %collective-permute-done.2), channel_id=1, source_target_pairs={{0,4},{4,8},{8,12},{12,16},{16,20},{20,24},{24,28},{28,0},{1,5},{5... | collective-permute-start | bytes 393224 | tf_op jit(solution)/shard_map/ppermute | solution.py:16
  62.1 8.3 %collective-permute-start.4 = (bf16[128,512]{1,0:T(8,128)(2,1)}, bf16[128,512]{1,0:T(8,128)(2,1)}, u32[]{:S(2)}, u32[]{:S(2)}) collective-permute-start(bf16[128,512]{1,0:T(8,128)(2,1)} %collective-permute-done.3), channel_id=1, source_target_pairs={{0,4},{4,8},{8,12},{12,16},{16,20},{20,24},{24,28},{28,0},{1,5},{5... | collective-permute-start | bytes 393224 | tf_op jit(solution)/shard_map/ppermute | solution.py:16
  70.4 7.9 %collective-permute-start.5 = (bf16[128,512]{1,0:T(8,128)(2,1)}, bf16[128,512]{1,0:T(8,128)(2,1)S(1)}, u32[]{:S(2)}, u32[]{:S(2)}) collective-permute-start(bf16[128,512]{1,0:T(8,128)(2,1)} %collective-permute-done.4), channel_id=1, source_target_pairs={{0,4},{4,8},{8,12},{12,16},{16,20},{20,24},{24,28},{28,0},{1,5},{5... | collective-permute-start | bytes 393224 | tf_op jit(solution)/shard_map/ppermute | solution.py:16
  78.3 9.6 %collective-permute-start.6 = (bf16[128,512]{1,0:T(8,128)(2,1)S(1)}, bf16[128,512]{1,0:T(8,128)(2,1)S(1)}, u32[]{:S(2)}, u32[]{:S(2)}) collective-permute-start(bf16[128,512]{1,0:T(8,128)(2,1)S(1)} %collective-permute-done.5), channel_id=1, source_target_pairs={{0,4},{4,8},{8,12},{12,16},{16,20},{20,24},{24,28},{28,0},{1,5},{5... | collective-permute-start | bytes 393224 | tf_op jit(solution)/shard_map/ppermute | solution.py:16
  101.1 103.8 %all-gather.5.cloned.1.call-start = ((), (), s32[]{:S(2)}) async-start(), calls=%async_computation.5 | async-start | bytes 1179648 | tf_op jit(solution)/shard_map/all_gather | solution.py:77
  101.1 34.9 %copy-start.24 = (f32[128]{0:T(128)}, f32[128]{0:T(128)S(1)}, u32[]{:S(2)}) copy-start(f32[128]{0:T(128)S(1)} %broadcast_add_fusion) | copy-start | bytes 1540
  136.0 76.0 %reduce-scatter.8.cloned.1.call-start = ((), (), s32[]{:S(2)}) async-start(), calls=%async_computation.7 | async-start | bytes 983040 | tf_op jit(solution)/shard_map/reduce_scatter | solution.py:146
  142.1 9.3 %collective-permute-start.7 = (bf16[128,512]{1,0:T(8,128)(2,1)S(1)}, bf16[128,512]{1,0:T(8,128)(2,1)S(1)}, u32[]{:S(2)}, u32[]{:S(2)}) collective-permute-start(bf16[128,512]{1,0:T(8,128)(2,1)S(1)} %fusion.50), channel_id=1, source_target_pairs={{0,4},{4,8},{8,12},{12,16},{16,20},{20,24},{24,28},{28,0},{1,5},{5... | collective-permute-start | bytes 393224 | tf_op jit(solution)/shard_map/ppermute | solution.py:16
  152.1 7.9 %collective-permute-start.8 = (bf16[128,512]{1,0:T(8,128)(2,1)S(1)}, bf16[128,512]{1,0:T(8,128)(2,1)S(1)}, u32[]{:S(2)}, u32[]{:S(2)}) collective-permute-start(bf16[128,512]{1,0:T(8,128)(2,1)S(1)} %collective-permute-done.7), channel_id=1, source_target_pairs={{0,4},{4,8},{8,12},{12,16},{16,20},{20,24},{24,28},{28,0},{1,5},{5... | collective-permute-start | bytes 393224 | tf_op jit(solution)/shard_map/ppermute | solution.py:16
  159.9 7.8 %collective-permute-start.9 = (bf16[128,512]{1,0:T(8,128)(2,1)S(1)}, bf16[128,512]{1,0:T(8,128)(2,1)S(1)}, u32[]{:S(2)}, u32[]{:S(2)}) collective-permute-start(bf16[128,512]{1,0:T(8,128)(2,1)S(1)} %collective-permute-done.8), channel_id=1, source_target_pairs={{0,4},{4,8},{8,12},{12,16},{16,20},{20,24},{24,28},{28,0},{1,5},{5... | collective-permute-start | bytes 393224 | tf_op jit(solution)/shard_map/ppermute | solution.py:16
  167.8 8.3 %collective-permute-start.10 = (bf16[128,512]{1,0:T(8,128)(2,1)S(1)}, bf16[128,512]{1,0:T(8,128)(2,1)}, u32[]{:S(2)}, u32[]{:S(2)}) collective-permute-start(bf16[128,512]{1,0:T(8,128)(2,1)S(1)} %collective-permute-done.9), channel_id=1, source_target_pairs={{0,4},{4,8},{8,12},{12,16},{16,20},{20,24},{24,28},{28,0},{1,5},{5... | collective-permute-start | bytes 393224 | tf_op jit(solution)/shard_map/ppermute | solution.py:16
  172.0 60.5 %reduce-scatter.6.cloned.1.call-start = ((), (), s32[]{:S(2)}) async-start(), calls=%async_computation.6 | async-start | bytes 983040 | tf_op jit(solution)/shard_map/reduce_scatter | solution.py:137
  176.1 8.0 %collective-permute-start.11 = (bf16[128,512]{1,0:T(8,128)(2,1)}, bf16[128,512]{1,0:T(8,128)(2,1)}, u32[]{:S(2)}, u32[]{:S(2)}) collective-permute-start(bf16[128,512]{1,0:T(8,128)(2,1)} %collective-permute-done.10), channel_id=1, source_target_pairs={{0,4},{4,8},{8,12},{12,16},{16,20},{20,24},{24,28},{28,0},{1,5},{5... | collective-permute-start | bytes 393224 | tf_op jit(solution)/shard_map/ppermute | solution.py:16
  184.1 7.9 %collective-permute-start.12 = (bf16[128,512]{1,0:T(8,128)(2,1)}, bf16[128,512]{1,0:T(8,128)(2,1)S(1)}, u32[]{:S(2)}, u32[]{:S(2)}) collective-permute-start(bf16[128,512]{1,0:T(8,128)(2,1)} %collective-permute-done.11), channel_id=1, source_target_pairs={{0,4},{4,8},{8,12},{12,16},{16,20},{20,24},{24,28},{28,0},{1,5},{5... | collective-permute-start | bytes 393224 | tf_op jit(solution)/shard_map/ppermute | solution.py:16
  191.9 7.7 %collective-permute-start.13 = (bf16[128,512]{1,0:T(8,128)(2,1)S(1)}, bf16[128,512]{1,0:T(8,128)(2,1)S(1)}, u32[]{:S(2)}, u32[]{:S(2)}) collective-permute-start(bf16[128,512]{1,0:T(8,128)(2,1)S(1)} %collective-permute-done.12), channel_id=1, source_target_pairs={{0,4},{4,8},{8,12},{12,16},{16,20},{20,24},{24,28},{28,0},{1,5},{5... | collective-permute-start | bytes 393224 | tf_op jit(solution)/shard_map/ppermute | solution.py:16
  210.4 63.3 %copy-start.23 = (s32[2]{0:T(128)S(1)}, s32[2]{0:T(128)}, u32[]{:S(2)}) copy-start(s32[2]{0:T(128)} %param.18) | copy-start | bytes 28
  (22 other events, 195.3 us)
Sparse Core Ops, SparseCore 0:
  49.9 43.5 all-gather.2
  101.2 21.6 reduce-scatter.3
  136.1 43.9 all-gather.4
  183.1 21.9 reduce-scatter.7
  212.1 20.3 reduce-scatter.5
